TPU v7x, 128 devices: a whole 4x4x4 slice. The times are simulated.
128 devices in a mesh: part: 1, row: 16 (over z, y), col: 8 (over x, core).
Axes of the slice: x: 4, y: 4, z: 4, core: 2. Of those that a mesh axis runs over, the one named last changes fastest.
Arguments:
- ratings: float32 [2048, 65536], P(('part', 'row'), 'col')
- mask: int32 [2048, 65536], P(('part', 'row'), 'col')
- user_init: float32 [2048, 128], P(('part', 'row'))
- item_init: float32 [65536, 128], P(('part', 'col'))
Outputs:
- output 1: float32 [2048, 128], P(('part', 'row'))
- output 2: float32 [65536, 128], P(('part', 'col'))
All inputs are finite; a program needn't handle non-finite values.
Results may differ from a plain program's by a relative error of at most 0.00267786.
Values are sent between devices in bfloat16 or wider.
A program may use at most 1 GiB of HBM per device.

v0:
```python
import jax
import jax.numpy as jnp
from jax import lax
from jax.sharding import PartitionSpec as P

CG_STEPS = 4
RIDGE_WEIGHT = 0.0005


def obs_scores(fixed_bf, moving_bf, by_rows):
    if by_rows:
        return lax.dot_general(moving_bf, fixed_bf, (((1,), (1,)), ((), ())), preferred_element_type=jnp.float32)
    return lax.dot_general(fixed_bf, moving_bf, (((1,), (1,)), ((), ())), preferred_element_type=jnp.float32)


def back_product(block_bf, fixed_bf, by_rows):
    contract = 1 if by_rows else 0
    return lax.dot_general(block_bf, fixed_bf, (((contract,), (0,)), ((), ())), preferred_element_type=jnp.float32)


def cg_block(mask_on, ratings_blk, fixed_fac, start, ridge, axis_name, by_rows):
    fixed_bf = fixed_fac.astype(jnp.bfloat16)
    scores = obs_scores(fixed_bf, start.astype(jnp.bfloat16), by_rows)
    resid_obs = jnp.where(mask_on, ratings_blk - scores, 0.0).astype(jnp.bfloat16)
    residual = lax.psum(back_product(resid_obs, fixed_bf, by_rows), axis_name) - ridge * start
    direction = residual
    estimate = start
    res_sq = jnp.sum(residual * residual, axis=1, keepdims=True)
    for cg_step in range(CG_STEPS):
        scores = obs_scores(fixed_bf, direction.astype(jnp.bfloat16), by_rows)
        masked = jnp.where(mask_on, scores.astype(jnp.bfloat16), 0.0)
        gram_dir = lax.psum(back_product(masked, fixed_bf, by_rows), axis_name) + ridge * direction
        step_size = res_sq / jnp.sum(direction * gram_dir, axis=1, keepdims=True)
        estimate = estimate + step_size * direction
        if cg_step + 1 < CG_STEPS:
            residual = residual - step_size * gram_dir
            new_sq = jnp.sum(residual * residual, axis=1, keepdims=True)
            direction = residual + (new_sq / res_sq) * direction
            res_sq = new_sq
    return estimate


def solution(mesh):
    row_size = mesh.shape["row"]
    col_size = mesh.shape["col"]
    grid_spec = P(("part", "row"), "col")
    user_spec = P(("part", "row"), None)
    item_spec = P(("part", "col"), None)

    def local_step(ratings_blk, mask_blk, user_blk, item_blk):
        users_part = ratings_blk.shape[0] * row_size
        items_part = ratings_blk.shape[1] * col_size
        mask_on = mask_blk > 0
        user_new = cg_block(mask_on, ratings_blk, item_blk, user_blk, RIDGE_WEIGHT * items_part, "col", True)
        item_new = cg_block(mask_on, ratings_blk, user_new, item_blk, RIDGE_WEIGHT * users_part, "row", False)
        return user_new, item_new

    return jax.shard_map(local_step, mesh=mesh, in_specs=(grid_spec, grid_spec, user_spec, item_spec), out_specs=(user_spec, item_spec), check_vma=False)
```

profile of v0, /device:TPU:0, one launch (start us, length us, event | category | flops | bytes accessed | tf_op | source)
XLA Modules:
  0.0 949.9 jit_solution(10134443140750431743)
XLA Ops:
  7.2 2.9 broadcast_compare_fusion
  10.1 0.6 copy-done.8
  10.9 0.6 copy-done.13
  11.5 4.1 fusion.33
  15.7 62.3 %all-reduce.11.cloned.1.call-done = f32[128,128]{1,0:T(8,128)} async-done(((f32[128,128]{1,0:T(8,128)}), f32[128,128]{1,0:T(8,128)}) %all-reduce.11.cloned.1.call-update) | async-done | bytes 65552 | tf_op jit(solution)/shard_map/psum | solution.py:25
  77.9 0.8 multiply_subtract_fusion.7
  78.8 1.9 fusion.32
  80.7 58.7 %all-reduce.13.cloned.1.call-done = f32[128,128]{1,0:T(8,128)} async-done(((f32[128,128]{1,0:T(8,128)}), f32[128,128]{1,0:T(8,128)}) %all-reduce.13.cloned.1.call-update) | async-done | bytes 65552 | tf_op jit(solution)/shard_map/psum | solution.py:32
  139.4 1.0 multiply_reduce_fusion.14
  140.5 1.0 multiply_reduce_fusion.13
  141.5 2.8 fusion.31
  144.4 58.6 %all-reduce.15.cloned.1.call-done = f32[128,128]{1,0:T(8,128)} async-done(((f32[128,128]{1,0:T(8,128)}), f32[128,128]{1,0:T(8,128)}) %all-reduce.15.cloned.1.call-update) | async-done | bytes 65552 | tf_op jit(solution)/shard_map/psum | solution.py:32
  203.0 1.0 multiply_reduce_fusion.12
  204.0 1.0 multiply_reduce_fusion.11
  205.1 0.6 copy-done.14
  205.8 1.9 fusion.30
  207.8 58.7 %all-reduce.17.cloned.1.call-done = f32[128,128]{1,0:T(8,128)} async-done(((f32[128,128]{1,0:T(8,128)}), f32[128,128]{1,0:T(8,128)}) %all-reduce.17.cloned.1.call-update) | async-done | bytes 65552 | tf_op jit(solution)/shard_map/psum | solution.py:32
  266.5 0.9 multiply_reduce_fusion.10
  267.4 1.1 multiply_reduce_fusion.9
  268.5 1.9 fusion.29
  270.5 58.7 %all-reduce.19.cloned.1.call-done = f32[128,128]{1,0:T(8,128)} async-done(((f32[128,128]{1,0:T(8,128)}), f32[128,128]{1,0:T(8,128)}) %all-reduce.19.cloned.1.call-update) | async-done | bytes 65552 | tf_op jit(solution)/shard_map/psum | solution.py:32
  329.2 1.0 multiply_reduce_fusion.8
  330.3 0.8 fusion.62
  331.1 5.6 fusion.28
  336.7 102.5 %all-reduce.21.cloned.1.call-done = f32[8192,128]{1,0:T(8,128)} async-done(((f32[8192,128]{1,0:T(8,128)}), f32[8192,128]{1,0:T(8,128)}) %all-reduce.21.cloned.1.call-update) | async-done | bytes 4194320 | tf_op jit(solution)/shard_map/psum | solution.py:25
  439.2 6.0 multiply_subtract_fusion.3
  445.2 5.4 fusion.26
  450.9 103.0 %all-reduce.23.cloned.1.call-done = f32[8192,128]{1,0:T(8,128)} async-done(((f32[8192,128]{1,0:T(8,128)}), f32[8192,128]{1,0:T(8,128)}) %all-reduce.23.cloned.1.call-update) | async-done | bytes 4194320 | tf_op jit(solution)/shard_map/psum | solution.py:32
  553.9 5.8 multiply_reduce_fusion.6
  559.9 2.3 multiply_reduce_fusion.5
  562.2 7.1 fusion.23
  569.4 103.2 %all-reduce.25.cloned.1.call-done = f32[8192,128]{1,0:T(8,128)} async-done(((f32[8192,128]{1,0:T(8,128)}), f32[8192,128]{1,0:T(8,128)}) %all-reduce.25.cloned.1.call-update) | async-done | bytes 4194320 | tf_op jit(solution)/shard_map/psum | solution.py:32
  672.6 7.5 multiply_reduce_fusion.4
  680.1 0.9 copy-done.11
  681.0 5.1 multiply_reduce_fusion.3
  686.1 1.9 copy-done.9
  688.1 6.5 multiply_add_fusion.3
  694.6 5.4 fusion.20
  700.3 103.0 %all-reduce.27.cloned.1.call-done = f32[8192,128]{1,0:T(8,128)} async-done(((f32[8192,128]{1,0:T(8,128)}), f32[8192,128]{1,0:T(8,128)}) %all-reduce.27.cloned.1.call-update) | async-done | bytes 4194320 | tf_op jit(solution)/shard_map/psum | solution.py:32
  803.3 4.8 multiply_reduce_fusion.2
  808.1 1.1 copy-done.10
  809.2 5.4 multiply_reduce_fusion.1
  814.6 6.0 fusion.17
  820.7 103.3 %all-reduce.29.cloned.1.call-done = f32[8192,128]{1,0:T(8,128)} async-done(((f32[8192,128]{1,0:T(8,128)}), f32[8192,128]{1,0:T(8,128)}) %all-reduce.29.cloned.1.call-update) | async-done | bytes 4194320 | tf_op jit(solution)/shard_map/psum | solution.py:32
  924.0 6.0 multiply_reduce_fusion
  930.0 1.1 copy-done.4
  931.1 1.2 copy-done.7
  932.3 10.8 %multiply_add_fusion = f32[8192,128]{1,0:T(8,128)} fusion(f32[8192,128]{1,0:T(8,128)S(1)} %copy-done.4, f32[8192,128]{1,0:T(8,128)} %param.7, f32[8192,128]{1,0:T(8,128)S(1)} %copy-done.2, f32[8192]{0:T(1024)S(1)} %div.125, f32[8192]{0:T(1024)S(1)} %div.123, f32[8192]{0:T(1024)S(1)} %div.121, f32[8192]{0:T(1024)S(1)} %div.119, ...), kind=kLoop, calls=%fused_computation.22 | loop fusion | flops 16777216 | bytes 25362432 | tf_op jit(solution)/shard_map/add | solution.py:34
  (58 shorter events, 1.5 us)
Async XLA Ops:
  7.2 70.8 %all-reduce.11.cloned.1.call-start = ((), (), s32[]{:S(2)}) async-start(), calls=%async_computation | async-start | bytes 131072 | tf_op jit(solution)/shard_map/psum | solution.py:25
  7.2 3.5 copy-start.8
  10.7 0.8 copy-start.13
  15.6 123.8 %all-reduce.13.cloned.1.call-start = ((), (), s32[]{:S(2)}) async-start(), calls=%async_computation.1 | async-start | bytes 131072 | tf_op jit(solution)/shard_map/psum | solution.py:32
  80.7 122.3 %all-reduce.15.cloned.1.call-start = ((), (), s32[]{:S(2)}) async-start(), calls=%async_computation.2 | async-start | bytes 131072 | tf_op jit(solution)/shard_map/psum | solution.py:32
  139.4 63.5 %copy-start.12 = (f32[128,128]{1,0:T(8,128)S(1)}, f32[128,128]{1,0:T(8,128)}, u32[]{:S(2)}) copy-start(f32[128,128]{1,0:T(8,128)} %all-reduce.13.cloned.1.call-done) | copy-start | bytes 196612
  144.3 122.2 %all-reduce.17.cloned.1.call-start = ((), (), s32[]{:S(2)}) async-start(), calls=%async_computation.3 | async-start | bytes 131072 | tf_op jit(solution)/shard_map/psum | solution.py:32
  205.1 0.6 copy-start.14
  207.7 121.5 %all-reduce.19.cloned.1.call-start = ((), (), s32[]{:S(2)}) async-start(), calls=%async_computation.4 | async-start | bytes 131072 | tf_op jit(solution)/shard_map/psum | solution.py:32
  270.5 168.7 %all-reduce.21.cloned.1.call-start = ((), (), s32[]{:S(2)}) async-start(), calls=%async_computation.5 | async-start | bytes 8388608 | tf_op jit(solution)/shard_map/psum | solution.py:25
  336.7 217.2 %all-reduce.23.cloned.1.call-start = ((), (), s32[]{:S(2)}) async-start(), calls=%async_computation.6 | async-start | bytes 8388608 | tf_op jit(solution)/shard_map/psum | solution.py:32
  450.7 221.9 %all-reduce.25.cloned.1.call-start = ((), (), s32[]{:S(2)}) async-start(), calls=%async_computation.7 | async-start | bytes 8388608 | tf_op jit(solution)/shard_map/psum | solution.py:32
  553.9 5.9 copy-start
  553.9 5.9 copy-start.5
  569.3 233.9 %all-reduce.27.cloned.1.call-start = ((), (), s32[]{:S(2)}) async-start(), calls=%async_computation.8 | async-start | bytes 8388608 | tf_op jit(solution)/shard_map/psum | solution.py:32
  672.6 7.5 copy-start.1
  672.6 7.5 copy-start.6
  672.6 8.4 copy-start.11
  686.1 2.0 copy-start.9
  700.0 223.9 %all-reduce.29.cloned.1.call-start = ((), (), s32[]{:S(2)}) async-start(), calls=%async_computation.9 | async-start | bytes 8388608 | tf_op jit(solution)/shard_map/psum | solution.py:32
  803.3 4.8 copy-start.3
  803.3 5.9 copy-start.10
  923.9 6.0 copy-start.2
  924.0 7.1 copy-start.4
  924.0 8.3 copy-start.7
Sparse Core Ops, SparseCore 0:
  15.7 62.1 all-reduce.10
  80.8 58.5 all-reduce.12
  144.4 58.4 all-reduce.14
  207.9 58.5 all-reduce.16
  270.6 58.5 all-reduce.18
  336.8 102.3 all-reduce.20
  450.8 103.1 all-reduce.22
  569.5 103.0 all-reduce.24
  700.1 103.0 all-reduce.26
  820.8 103.1 all-reduce.28
where the time goes:
time: 951 us; the launch traced here: 950 us
  waiting for transfers between devices  812 us (85%)
  other arithmetic  72.2 us (8%)
  matrix products  42.1 us (4%)
  between operations  14.4 us (2%)
    psum x8, waiting for transfers between devices, cg_block(): lax.psum(back_product(masked, fixed_bf, by_rows), axis_name)  647 us
    psum x2, waiting for transfers between devices, cg_block(): lax.psum(back_product(resid_obs, fixed_bf, by_rows), axis_name)  165 us
    dot_general x10, matrix products, back_product(): lax.dot_general(block_bf, fixed_bf, (((contract,), (0,)), ((), ())), pref...  42.1 us
    reduce_sum x8, other arithmetic, cg_block(): step_size = res_sq / jnp.sum(direction * gram_dir, axis=1, keepdims=True)  28 us
  transfers between devices with their start and end apart: 10, of which 10 were waited for; matrix products, arithmetic and copies ran while one was open for 0% of the time, Pallas kernels for 0%

commit v1 on v0

v1 whole, which is shorter than its diff:
```python
import jax
import jax.numpy as jnp
from jax import lax
from jax.experimental import pallas as pl
from jax.experimental.pallas import tpu as pltpu
from jax.sharding import PartitionSpec as P

CG_STEPS = 4
RIDGE_WEIGHT = 0.0005
MESH = pl.DeviceIdType.MESH
F32 = jnp.float32
BF16 = jnp.bfloat16

NZ = NY = 4
NROW = NZ * NY
NCOL = 8
CHUNKS = 2
OFFSETS = sorted(
    [(dz, dy) for dz in range(NZ) for dy in range(NY) if dz or dy],
    key=lambda o: min(o[0], NZ - o[0]) + min(o[1], NY - o[1]),
)


def dot(a, b, ca, cb):
    return lax.dot_general(a, b, (((ca,), (cb,)), ((), ())), preferred_element_type=F32)


def kernel(
    ratings, mask, user_init, item_init, user_out, item_out,
    r_in, m_in, v_in, w_in, fixed, mask_bf, r_send, r_recv, mask_items,
    part_sums, rs_recv, p_all, w_all, fw, fw_t, v_all,
    in_sem, w_in_sem, v_in_sem, a2a_send, a2a_recv, rs_send_sem, rs_recv_sem, ag_send, ag_recv,
    wc_send, wc_recv, wr_send, wr_recv, vg_send, vg_recv, out_sem, wout_sem,
):
    users, items = r_in.shape
    rank = w_in.shape[1]
    own_users = users // NCOL
    own_items = items // NROW
    all_users = users * NROW
    row = lax.axis_index("row")
    col = lax.axis_index("col")
    zi = row // NY
    yi = lax.rem(row, NY)
    ridge_user = RIDGE_WEIGHT * items * NCOL
    ridge_item = RIDGE_WEIGHT * all_users

    def row_of(dz, dy):
        return lax.rem(zi + dz, NZ) * NY + lax.rem(yi + dy, NY)

    def row_dev(r):
        return (0, r, col)

    def col_dev(k):
        return (0, row, lax.rem(col + k, NCOL))

    def remote(src, dst, send, recv, dev):
        return pltpu.make_async_remote_copy(
            src_ref=src, dst_ref=dst, send_sem=send, recv_sem=recv, device_id=dev, device_id_type=MESH
        )

    barrier = pltpu.get_barrier_semaphore()
    for dz, dy in OFFSETS:
        pl.semaphore_signal(barrier, inc=1, device_id=row_dev(row_of(dz, dy)), device_id_type=MESH)
    for k in range(1, NCOL):
        pl.semaphore_signal(barrier, inc=1, device_id=col_dev(k), device_id_type=MESH)

    order = OFFSETS + [(0, 0)]
    loads = []
    for k, (dz, dy) in enumerate(order):
        cols = pl.ds(pl.multiple_of(row_of(dz, dy) * own_items, own_items), own_items)
        a = pltpu.make_async_copy(ratings.at[:, cols], r_in.at[:, cols], in_sem.at[0, k])
        b = pltpu.make_async_copy(mask.at[:, cols], m_in.at[:, cols], in_sem.at[1, k])
        a.start()
        b.start()
        loads.append((a, b, cols))
    w_load = pltpu.make_async_copy(user_init, w_in, w_in_sem)
    w_load.start()
    v_load = pltpu.make_async_copy(item_init, v_in, v_in_sem)
    v_load.start()

    pl.semaphore_wait(barrier, len(OFFSETS) + NCOL - 1)

    my_users = pl.ds(pl.multiple_of(row * users, users), users)
    exchange = []
    for k, (dz, dy) in enumerate(order):
        a, b, cols = loads[k]
        a.wait()
        b.wait()
        on = m_in[:, cols] > 0
        mask_bf[:, cols] = on.astype(F32).astype(BF16)
        marked = jnp.where(on, r_in[:, cols], jnp.inf)
        if (dz, dy) == (0, 0):
            r_recv[my_users, :] = marked
        else:
            r_send[k] = marked
            c = remote(r_send.at[k], r_recv.at[my_users, :], a2a_send.at[k], a2a_recv.at[k], row_dev(row_of(dz, dy)))
            c.start()
            exchange.append(c)

    w_load.wait()
    v_load.wait()
    tile = items // 8
    fixed[...] = v_in[...].astype(BF16)

    def reduce_users(it, acc):
        part_sums[it] = acc
        copies = []
        for k in range(1, NCOL):
            peer = lax.rem(col + k, NCOL)
            c = remote(
                part_sums.at[it, pl.ds(pl.multiple_of(peer * own_users, own_users), own_users)],
                rs_recv.at[it, k - 1], rs_send_sem.at[it, k - 1], rs_recv_sem.at[it, k - 1], col_dev(k),
            )
            c.start()
            copies.append(c)
        total = part_sums[it, mine, :]
        for k in range(1, NCOL):
            copies[k - 1].wait()
            total = total + rs_recv[it, k - 1]
        return total

    def share_direction(it, p):
        p_all[it, mine, :] = p.astype(BF16)
        copies = []
        for k in range(1, NCOL):
            c = remote(
                p_all.at[it, mine], p_all.at[it, mine], ag_send.at[it, k - 1], ag_recv.at[it, k - 1], col_dev(k)
            )
            c.start()
            copies.append(c)
        for c in copies:
            c.wait()

    def user_product(it):
        p = p_all[it]
        acc = jnp.zeros((users, rank), F32)
        for t in range(8):
            f = fixed[t * tile:(t + 1) * tile, :]
            z = dot(p, f, 1, 1).astype(BF16) * mask_bf[:, t * tile:(t + 1) * tile]
            acc = acc + dot(z, f, 1, 0)
        return acc

    mine = pl.ds(pl.multiple_of(col * own_users, own_users), own_users)
    w_bf = w_in[...].astype(BF16)
    acc = jnp.zeros((users, rank), F32)
    for t in range(8):
        cols = slice(t * tile, (t + 1) * tile)
        f = fixed[cols, :]
        d = jnp.where(m_in[:, cols] > 0, r_in[:, cols] - dot(w_bf, f, 1, 1), 0.0).astype(BF16)
        acc = acc + dot(d, f, 1, 0)
    x = w_in[mine, :]
    r = reduce_users(0, acc) - ridge_user * x
    p = r
    rr = jnp.sum(r * r, axis=1, keepdims=True)
    share_direction(0, p)

    def user_step(it, state):
        x, r, p, rr = state
        q = reduce_users(it, user_product(it - 1)) + ridge_user * p
        a = rr / jnp.sum(p * q, axis=1, keepdims=True)
        x = x + a * p
        r = r - a * q
        rn = jnp.sum(r * r, axis=1, keepdims=True)
        p = r + (rn / rr) * p
        share_direction(it, p)
        return x, r, p, rn

    x, r, p, rr = lax.fori_loop(1, CG_STEPS, user_step, (x, r, p, rr))
    q = reduce_users(CG_STEPS, user_product(CG_STEPS - 1)) + ridge_user * p
    a = rr / jnp.sum(p * q, axis=1, keepdims=True)
    x = x + a * p

    w_all[mine, :] = x
    copies = []
    for k in range(1, NCOL):
        c = remote(w_all.at[mine], w_all.at[mine], wc_send.at[k - 1], wc_recv.at[k - 1], col_dev(k))
        c.start()
        copies.append(c)
    for c in copies:
        c.wait()
    w_out = pltpu.make_async_copy(w_all, user_out, wout_sem)
    w_out.start()
    fw[my_users, :] = w_all[...].astype(BF16)
    shared = []
    for k, (dz, dy) in enumerate(OFFSETS):
        c = remote(fw.at[my_users], fw.at[my_users], wr_send.at[k], wr_recv.at[k], row_dev(row_of(dz, dy)))
        c.start()
        shared.append(c)

    for c in exchange:
        c.wait()
    step = all_users // 8
    for t in range(8):
        rows = slice(t * step, (t + 1) * step)
        mask_items[rows, :] = jnp.where(r_recv[rows, :] < jnp.inf, 1.0, 0.0).astype(BF16)
    x_all = v_in[pl.ds(pl.multiple_of(row * own_items, own_items), own_items), :].T
    for c in shared:
        c.wait()
    fw_t[...] = fw[...].astype(F32).T.astype(BF16)

    width = own_items // CHUNKS
    half = width // 2
    tall = all_users // 4

    def item_product(p_bf, cols, first):
        acc = jnp.zeros((rank, width), F32)
        for t in range(4):
            rows = slice(t * tall, (t + 1) * tall)
            s = dot(fw[rows, :], p_bf, 1, 0)
            if first:
                known = r_recv[rows, cols]
                z = jnp.where(known < jnp.inf, known - s, 0.0).astype(BF16)
            else:
                z = s.astype(BF16) * mask_items[rows, cols]
            acc = acc + dot(fw_t[:, rows], z, 1, 0)
        return acc

    def block(r, q, h):
        return pl.ds(pl.multiple_of(r * own_items + q * width + h * half, half), half)

    def halfblock(r, q, h, part):
        n = half // 2
        return pl.ds(pl.multiple_of(r * own_items + q * width + h * half + part * n, n), n)

    dims = [((0, 1), (1, 0)), ((1, 0), (0, 1))]

    def scaled(d, n):
        return (d[0] * n % NZ, d[1] * n % NY)

    def added(d, e):
        return ((d[0] + e[0]) % NZ, (d[1] + e[1]) % NY)

    started = []

    def send(rows, dev, q, h, slot):
        c = remote(v_all.at[rows], v_all.at[rows], vg_send.at[q, h, slot], vg_recv.at[q, h, slot], dev)
        c.start()
        started.append(c)
        return c

    def gather_own(q):
        got = {}
        for h in range(2):
            d1, d2 = dims[h]
            for s, sign in enumerate((1, 3)):
                got[h, 0, s] = send(block(row, q, h), row_dev(row_of(*scaled(d1, sign))), q, h, s)
            for s, sign in enumerate((1, 3)):
                got[h, 1, 0, s] = send(block(row, q, h), row_dev(row_of(*scaled(d2, sign))), q, h, 4 + s)
        return got

    def gather_first(q, got):
        for s, sign in enumerate((1, 3)):
            for h in range(2):
                d1, d2 = dims[h]
                got[h, 0, s].wait_recv()
                src = row_of(*scaled(d1, 4 - sign))
                got[h, 2, s] = send(
                    halfblock(src, q, h, s), row_dev(row_of(*scaled(d1, sign))), q, h, 2 + s
                )
                for s2, sign2 in enumerate((1, 3)):
                    got[h, 1, 1 + s, s2] = send(
                        block(src, q, h), row_dev(row_of(*scaled(d2, sign2))), q, h, 6 + 2 * s + s2
                    )
        for h in range(2):
            d1, d2 = dims[h]
            got[h, 2, 0].wait_recv()
            got[h, 2, 1].wait_recv()
            src = row_of(*scaled(d1, 2))
            for s2, sign2 in enumerate((1, 3)):
                got[h, 1, 3, s2] = send(block(src, q, h), row_dev(row_of(*scaled(d2, sign2))), q, h, 10 + s2)

    def gather_second(q, got, b):
        for h in range(2):
            d1, d2 = dims[h]
            base = scaled(d1, (0, 3, 1, 2)[b])
            for s, sign in enumerate((1, 3)):
                got[h, 1, b, s].wait_recv()
                src = row_of(*added(base, scaled(d2, 4 - sign)))
                got[h, 3, b, s] = send(
                    halfblock(src, q, h, s), row_dev(row_of(*scaled(d2, sign))), q, h, 12 + 2 * b + s
                )

    pending = []
    for q in range(CHUNKS):
        cols = slice(q * width, (q + 1) * width)
        x = x_all[:, cols]
        r = item_product(x.astype(BF16), cols, True) - ridge_item * x
        p = r
        rr = jnp.sum(r * r, axis=0, keepdims=True)

        def item_step(_, state):
            x, r, p, rr = state
            q = item_product(p.astype(BF16), cols, False) + ridge_item * p
            a = rr / jnp.sum(p * q, axis=0, keepdims=True)
            x = x + a * p
            r = r - a * q
            rn = jnp.sum(r * r, axis=0, keepdims=True)
            p = r + (rn / rr) * p
            return x, r, p, rn

        x, r, p, rr = lax.fori_loop(0, CG_STEPS - 1, item_step, (x, r, p, rr))
        qv = item_product(p.astype(BF16), cols, False) + ridge_item * p
        x = x + rr / jnp.sum(p * qv, axis=0, keepdims=True) * p
        v_all[pl.ds(pl.multiple_of(row * own_items + q * width, width), width), :] = x.T
        pending.append(gather_own(q))

    for q in range(CHUNKS):
        gather_first(q, pending[q])
    for b in range(4):
        for q in range(CHUNKS):
            gather_second(q, pending[q], b)
    for q in range(CHUNKS):
        for h in range(2):
            for b in range(4):
                for s in range(2):
                    pending[q][h, 3, b, s].wait_recv()
    for c in started:
        c.wait_send()
    v_out = pltpu.make_async_copy(v_all, item_out, out_sem)
    v_out.start()
    v_out.wait()
    w_out.wait()


def solution(mesh):
    grid_spec = P(("part", "row"), "col")
    user_spec = P(("part", "row"), None)
    item_spec = P(("part", "col"), None)

    def local_step(ratings, mask, user_init, item_init):
        users, items = ratings.shape
        rank = user_init.shape[1]
        own_users = users // NCOL
        own_items = items // NROW
        all_users = users * NROW
        peers = len(OFFSETS)
        dma = pltpu.SemaphoreType.DMA
        hbm = pl.BlockSpec(memory_space=pl.ANY)
        return pl.pallas_call(
            kernel,
            out_shape=(
                jax.ShapeDtypeStruct((users, rank), F32),
                jax.ShapeDtypeStruct((items, rank), F32),
            ),
            in_specs=[hbm] * 4,
            out_specs=(hbm, hbm),
            scratch_shapes=[
                pltpu.VMEM((users, items), F32),
                pltpu.VMEM((users, items), jnp.int32),
                pltpu.VMEM((items, rank), F32),
                pltpu.VMEM((users, rank), F32),
                pltpu.VMEM((items, rank), BF16),
                pltpu.VMEM((users, items), BF16),
                pltpu.VMEM((peers, users, own_items), F32),
                pltpu.VMEM((all_users, own_items), F32),
                pltpu.VMEM((all_users, own_items), BF16),
                pltpu.VMEM((CG_STEPS + 1, users, rank), F32),
                pltpu.VMEM((CG_STEPS + 1, NCOL - 1, own_users, rank), F32),
                pltpu.VMEM((CG_STEPS, users, rank), BF16),
                pltpu.VMEM((users, rank), F32),
                pltpu.VMEM((all_users, rank), BF16),
                pltpu.VMEM((rank, all_users), BF16),
                pltpu.VMEM((items, rank), F32),
                dma((2, NROW)),
                dma,
                dma,
                dma((peers,)),
                dma((peers,)),
                dma((CG_STEPS + 1, NCOL - 1)),
                dma((CG_STEPS + 1, NCOL - 1)),
                dma((CG_STEPS, NCOL - 1)),
                dma((CG_STEPS, NCOL - 1)),
                dma((NCOL - 1,)),
                dma((NCOL - 1,)),
                dma((peers,)),
                dma((peers,)),
                dma((CHUNKS, 2, 20)),
                dma((CHUNKS, 2, 20)),
                dma,
                dma,
            ],
            compiler_params=pltpu.CompilerParams(
                collective_id=0, has_side_effects=True, vmem_limit_bytes=60 * 2**20
            ),
            name="als_sweep",
        )(ratings, mask, user_init, item_init)

    return jax.shard_map(
        local_step,
        mesh=mesh,
        in_specs=(grid_spec, grid_spec, user_spec, item_spec),
        out_specs=(user_spec, item_spec),
        check_vma=False,
    )
```

time: 951 us -> 123 us (0.13)
  waiting for transfers between devices: 812 us -> 0 us
  Pallas kernels: 0 us -> 117 us
  other arithmetic: 72.2 us -> 0 us
  matrix products: 42.1 us -> 0 us
  between operations: 14.4 us -> 0.64 us
    psum x10 -> x0, waiting for transfers between devices: 812 us -> none  [the longest x8 647 us: cg_block(): lax.psum(back_product(masked, fixed_bf, by_rows), axis_name)]
    pallas_call x0 -> x1, Pallas kernels: none -> 117 us  [local_step(): pl.pallas_call(kernel, out_shape=(jax.ShapeDtypeStruct((users, rank), F32...]
    reduce_sum x14 -> x0, other arithmetic: 44 us -> none  [the longest x8 28 us: cg_block(): step_size = res_sq / jnp.sum(direction * gram_dir, axis=1, keepdims=True)]
    dot_general x10 -> x0, matrix products: 42.1 us -> none  [back_product(): lax.dot_general(block_bf, fixed_bf, (((contract,), (0,)), ((), ())), pref...]
    add x3 -> x0, other arithmetic: 17.4 us -> none  [the longest x1 10.8 us: cg_block(): estimate = estimate + step_size * direction]
  transfers between devices with their start and end apart: 10 -> 0, of which waited for: 10 -> 0; matrix products, arithmetic and copies ran while one was open for 0% -> 0% of each run, Pallas kernels for 0% -> 0%
where the time goes in v1:
time: 123 us
  Pallas kernels  117 us (95%)
  local copies, waits for them, and re-layouts  5.94 us (5%)
    pallas_call x1, Pallas kernels, local_step(): pl.pallas_call(kernel, out_shape=(jax.ShapeDtypeStruct((users, rank), F32...  117 us
    unnamed x2, local copies, waits for them, and re-layouts  5.94 us

profile of v1, /device:TPU:0, one launch (start us, length us, event | category | flops | bytes accessed | tf_op | source)
XLA Modules:
  0.0 123.2 jit_solution(6180373349960241400)
XLA Ops:
  0.6 116.6 %als_sweep.1 = (f32[128,128]{1,0:T(8,128)}, f32[8192,128]{1,0:T(8,128)}) custom-call(f32[128,8192]{1,0:T(8,128)} %ratings.1, s32[128,8192]{1,0:T(8,128)} %mask.1, f32[128,128]{1,0:T(8,128)} %user_init.1, f32[8192,128]{1,0:T(8,128)} %item_init.1), custom_call_target="tpu_custom_call" | custom-call | tf_op jit(solution)/shard_map/als_sweep/pallas_call | solution.py:339
  117.2 1.5 %copy.8 = f32[128,128]{1,0:T(8,128)} copy(f32[128,128]{1,0:T(8,128)} %get-tuple-element.4) | data formatting | bytes 131072
  118.7 4.5 %copy.9 = f32[8192,128]{1,0:T(8,128)} copy(f32[8192,128]{1,0:T(8,128)} %get-tuple-element.5) | data formatting | bytes 8388608

commit v2 on v1

v2 whole, which is shorter than its diff:
```python
import jax
import jax.numpy as jnp
from jax import lax
from jax.experimental import pallas as pl
from jax.experimental.pallas import tpu as pltpu
from jax.sharding import PartitionSpec as P

CG_STEPS = 4
RIDGE_WEIGHT = 0.0005
MESH = pl.DeviceIdType.MESH
F32 = jnp.float32
BF16 = jnp.bfloat16

NZ = NY = 4
NROW = NZ * NY
NX = 4
NCOL = NX * 2
CHUNKS = 2
OFFSETS = [
    (1, 1), (3, 3), (1, 0), (3, 0), (2, 1), (2, 3), (2, 0), (1, 3), (3, 1), (1, 2), (3, 2), (2, 2), (0, 1), (0, 3), (0, 2),
]
NEAR_FIRST = sorted(
    range(len(OFFSETS)), key=lambda k: min(OFFSETS[k][0], NZ - OFFSETS[k][0]) + min(OFFSETS[k][1], NY - OFFSETS[k][1])
)


def dot(a, b, ca, cb):
    return lax.dot_general(a, b, (((ca,), (cb,)), ((), ())), preferred_element_type=F32)


def kernel(
    ratings, mask, user_init, item_init, user_out, item_out,
    r_in, m_in, v_in, w_in, fixed, fixed_t, mask_bf, r_send, r_recv, mask_items,
    pair_send, pair_recv, chip_sum, x_recv, p_all, fw, fw_t,
    in_sem, w_in_sem, v_in_sem, a2a_send, a2a_recv, pair_send_sem, pair_recv_sem, x_send_sem, x_recv_sem,
    ag_send, ag_recv, wc_send, wc_recv, wr_send, wr_recv, wf_send, wf_recv, vg_send, vg_recv,
):
    users, items = r_in.shape
    rank = w_in.shape[1]
    half_users = users // 2
    own_items = items // NROW
    all_users = users * NROW
    width = own_items // CHUNKS
    half = width // 2
    tall = all_users // 4
    tile = items // 8
    row = lax.axis_index("row")
    col = lax.axis_index("col")
    zi = row // NY
    yi = lax.rem(row, NY)
    xi = col // 2
    core = lax.rem(col, 2)
    ridge_user = RIDGE_WEIGHT * items * NCOL
    ridge_item = RIDGE_WEIGHT * all_users
    partner = (0, row, xi * 2 + 1 - core)

    def row_of(dz, dy):
        return lax.rem(zi + dz, NZ) * NY + lax.rem(yi + dy, NY)

    def row_dev(r):
        return (0, r, col)

    def x_dev(k):
        return (0, row, lax.rem(xi + k, NX) * 2 + core)

    def remote(src, dst, send, recv, dev):
        return pltpu.make_async_remote_copy(
            src_ref=src, dst_ref=dst, send_sem=send, recv_sem=recv, device_id=dev, device_id_type=MESH
        )

    peers = [row_dev(row_of(dz, dy)) for dz, dy in OFFSETS] + [x_dev(k) for k in range(1, NX)] + [partner]
    barrier = pltpu.get_barrier_semaphore()
    for dev in peers:
        pl.semaphore_signal(barrier, inc=1, device_id=dev, device_id_type=MESH)

    order = OFFSETS + [(0, 0)]
    loads = []
    for k, (dz, dy) in enumerate(order):
        cols = pl.ds(pl.multiple_of(row_of(dz, dy) * own_items, own_items), own_items)
        a = pltpu.make_async_copy(ratings.at[:, cols], r_in.at[:, cols], in_sem.at[0, k])
        b = pltpu.make_async_copy(mask.at[:, cols], m_in.at[:, cols], in_sem.at[1, k])
        a.start()
        b.start()
        loads.append((a, b, cols))
    w_load = pltpu.make_async_copy(user_init, w_in, w_in_sem)
    w_load.start()
    v_loads = []
    for t in range(8):
        c = pltpu.make_async_copy(
            item_init.at[t * tile:(t + 1) * tile], v_in.at[t * tile:(t + 1) * tile], v_in_sem.at[t]
        )
        c.start()
        v_loads.append(c)

    my_users = pl.ds(pl.multiple_of(row * users, users), users)
    exchange = {}

    def exchange_start(k, q):
        dz, dy = order[k]
        c = remote(
            r_send.at[q, k], r_recv.at[q, my_users, :], a2a_send.at[q, k], a2a_recv.at[q, k],
            row_dev(row_of(dz, dy)),
        )
        c.start()
        exchange[q, k] = c

    ahead = 4
    for k, (dz, dy) in enumerate(order):
        a, b, cols = loads[k]
        a.wait()
        b.wait()
        on = m_in[:, cols] > 0
        mask_bf[:, cols] = on.astype(F32).astype(BF16)
        marked = jnp.where(on, r_in[:, cols], jnp.inf)
        for q in range(CHUNKS):
            if (dz, dy) == (0, 0):
                r_recv[q, my_users, :] = marked[:, q * width:(q + 1) * width]
            else:
                r_send[q, k] = marked[:, q * width:(q + 1) * width]
        if k == ahead - 1:
            pl.semaphore_wait(barrier, len(peers))
            for j in range(ahead):
                exchange_start(j, 0)
        elif k >= ahead and k < len(OFFSETS):
            exchange_start(k, 0)
    for q in range(1, CHUNKS):
        for k in range(len(OFFSETS)):
            exchange_start(k, q)

    mine = pl.ds(pl.multiple_of(core * half_users, half_users), half_users)
    other = pl.ds(pl.multiple_of((1 - core) * half_users, half_users), half_users)

    def reduce_users(it, product, meanwhile=None):
        pair_send[it] = product(other)
        c = remote(pair_send.at[it], pair_recv.at[it], pair_send_sem.at[it], pair_recv_sem.at[it], partner)
        c.start()
        own = product(mine)
        c.wait()
        own = own + pair_recv[it]
        chip_sum[it] = own
        copies = []
        for k in (2, 1, 3):
            c = remote(
                chip_sum.at[it], x_recv.at[it, k - 1], x_send_sem.at[it, k - 1], x_recv_sem.at[it, k - 1], x_dev(k)
            )
            c.start()
            copies.append(c)
        if meanwhile is not None:
            meanwhile()
        for c in copies:
            c.wait()
        return (own + x_recv[it, 1]) + (x_recv[it, 0] + x_recv[it, 2])

    def share_direction(it, p):
        p_all[it, mine, :] = p.astype(BF16)
        c = remote(p_all.at[it, mine], p_all.at[it, mine], ag_send.at[it], ag_recv.at[it], partner)
        c.start()
        c.wait()

    def user_product(it):
        def product(rows):
            p = p_all[it, rows, :]
            acc = jnp.zeros((half_users, rank), F32)
            for t in range(8):
                cols = slice(t * tile, (t + 1) * tile)
                z = dot(p, fixed_t[:, cols], 1, 0).astype(BF16) * mask_bf[rows, cols]
                acc = acc + dot(z, fixed[cols, :], 1, 0)
            return acc
        return product

    w_load.wait()
    ready = []

    def user_residual(rows):
        w = w_in[rows, :].astype(BF16)
        acc = jnp.zeros((half_users, rank), F32)
        for t in range(8):
            cols = slice(t * tile, (t + 1) * tile)
            if len(ready) <= t:
                v_loads[t].wait()
                fixed[cols, :] = v_in[cols, :].astype(BF16)
                ready.append(t)
            f = fixed[cols, :]
            d = jnp.where(m_in[rows, cols] > 0, r_in[rows, cols] - dot(w, f, 1, 1), 0.0).astype(BF16)
            acc = acc + dot(d, f, 1, 0)
        return acc

    def transpose_fixed():
        for t in range(8):
            cols = slice(t * tile, (t + 1) * tile)
            fixed_t[:, cols] = fixed[cols, :].T

    x = w_in[mine, :]
    r = reduce_users(0, user_residual, transpose_fixed) - ridge_user * x
    p = r
    rr = jnp.sum(r * r, axis=1, keepdims=True)
    share_direction(0, p)

    def user_step(it, state):
        x, r, p, rr = state
        q = reduce_users(it, user_product(it - 1)) + ridge_user * p
        a = rr / jnp.sum(p * q, axis=1, keepdims=True)
        x = x + a * p
        r = r - a * q
        rn = jnp.sum(r * r, axis=1, keepdims=True)
        p = r + (rn / rr) * p
        share_direction(it, p)
        return x, r, p, rn

    x, r, p, rr = lax.fori_loop(1, CG_STEPS, user_step, (x, r, p, rr))
    q = reduce_users(CG_STEPS, user_product(CG_STEPS - 1)) + ridge_user * p
    a = rr / jnp.sum(p * q, axis=1, keepdims=True)
    x = x + a * p

    def user_block(r):
        return pl.ds(pl.multiple_of(r * users + core * half_users, half_users), half_users)

    fw[user_block(row), :] = x.astype(BF16)
    shared = {}
    for k in reversed(NEAR_FIRST):
        blk = user_block(row)
        c = remote(fw.at[blk], fw.at[blk], wr_send.at[k], wr_recv.at[k], row_dev(row_of(*OFFSETS[k])))
        c.start()
        shared[k] = c
    crossed = [remote(fw.at[user_block(row)], fw.at[user_block(row)], wf_send.at[NROW - 1], wf_recv.at[NROW - 1], partner)]
    crossed[0].start()
    user_out[mine, :] = x
    w_copy = remote(user_out.at[mine], user_out.at[mine], wc_send, wc_recv, partner)
    w_copy.start()

    def item_mask(q):
        for k in range(len(OFFSETS)):
            exchange[q, k].wait()
        for t in range(4):
            rows = slice(t * tall, (t + 1) * tall)
            mask_items[q, rows, :] = jnp.where(r_recv[q, rows, :] < jnp.inf, 1.0, 0.0).astype(BF16)

    x_all = v_in[pl.ds(pl.multiple_of(row * own_items, own_items), own_items), :].T
    item_mask(0)
    sources = [row]
    for k in NEAR_FIRST:
        shared[k].wait()
        src = row_of(NZ - OFFSETS[k][0], NY - OFFSETS[k][1])
        c = remote(fw.at[user_block(src)], fw.at[user_block(src)], wf_send.at[k], wf_recv.at[k], partner)
        c.start()
        crossed.append(c)
        sources.append(src)
    for c, src in zip(crossed, sources):
        c.wait()
        blk = pl.ds(pl.multiple_of(src * users, users), users)
        fw_t[:, blk] = fw[blk, :].T

    def item_product(p_bf, q, first):
        acc = jnp.zeros((rank, width), F32)
        for t in range(4):
            rows = slice(t * tall, (t + 1) * tall)
            s = dot(fw[rows, :], p_bf, 1, 0)
            if first:
                known = r_recv[q, rows, :]
                z = jnp.where(known < jnp.inf, known - s, 0.0).astype(BF16)
            else:
                z = s.astype(BF16) * mask_items[q, rows, :]
            acc = acc + dot(fw_t[:, rows], z, 1, 0)
        return acc

    def block(r, q, h):
        return pl.ds(pl.multiple_of(r * own_items + q * width + h * half, half), half)

    def halfblock(r, q, h, part):
        n = half // 2
        return pl.ds(pl.multiple_of(r * own_items + q * width + h * half + part * n, n), n)

    dims = [((0, 1), (1, 0)), ((1, 0), (0, 1))]

    def scaled(d, n):
        return (d[0] * n % NZ, d[1] * n % NY)

    def added(d, e):
        return ((d[0] + e[0]) % NZ, (d[1] + e[1]) % NY)

    started = []

    def send(rows, dev, q, h, slot):
        c = remote(item_out.at[rows], item_out.at[rows], vg_send.at[q, h, slot], vg_recv.at[q, h, slot], dev)
        c.start()
        started.append(c)
        return c

    def gather_own(q):
        got = {}
        for h in range(2):
            d1, d2 = dims[h]
            for s, sign in enumerate((1, 3)):
                got[h, 0, s] = send(block(row, q, h), row_dev(row_of(*scaled(d1, sign))), q, h, s)
            for s, sign in enumerate((1, 3)):
                got[h, 1, 0, s] = send(block(row, q, h), row_dev(row_of(*scaled(d2, sign))), q, h, 4 + s)
        return got

    def gather_first(q, got):
        for s, sign in enumerate((1, 3)):
            for h in range(2):
                d1, d2 = dims[h]
                got[h, 0, s].wait_recv()
                src = row_of(*scaled(d1, 4 - sign))
                got[h, 2, s] = send(
                    halfblock(src, q, h, s), row_dev(row_of(*scaled(d1, sign))), q, h, 2 + s
                )
                for s2, sign2 in enumerate((1, 3)):
                    got[h, 1, 1 + s, s2] = send(
                        block(src, q, h), row_dev(row_of(*scaled(d2, sign2))), q, h, 6 + 2 * s + s2
                    )
        for h in range(2):
            d1, d2 = dims[h]
            got[h, 2, 0].wait_recv()
            got[h, 2, 1].wait_recv()
            src = row_of(*scaled(d1, 2))
            for s2, sign2 in enumerate((1, 3)):
                got[h, 1, 3, s2] = send(block(src, q, h), row_dev(row_of(*scaled(d2, sign2))), q, h, 10 + s2)

    def gather_second(q, got, b):
        for h in range(2):
            d1, d2 = dims[h]
            base = scaled(d1, (0, 3, 1, 2)[b])
            for s, sign in enumerate((1, 3)):
                got[h, 1, b, s].wait_recv()
                src = row_of(*added(base, scaled(d2, 4 - sign)))
                got[h, 3, b, s] = send(
                    halfblock(src, q, h, s), row_dev(row_of(*scaled(d2, sign))), q, h, 12 + 2 * b + s
                )

    pending = []
    for q in range(CHUNKS):
        if q:
            item_mask(q)
        x = x_all[:, q * width:(q + 1) * width]
        r = item_product(x.astype(BF16), q, True) - ridge_item * x
        p = r
        rr = jnp.sum(r * r, axis=0, keepdims=True)

        def item_step(_, state):
            x, r, p, rr = state
            g = item_product(p.astype(BF16), q, False) + ridge_item * p
            a = rr / jnp.sum(p * g, axis=0, keepdims=True)
            x = x + a * p
            r = r - a * g
            rn = jnp.sum(r * r, axis=0, keepdims=True)
            p = r + (rn / rr) * p
            return x, r, p, rn

        x, r, p, rr = lax.fori_loop(0, CG_STEPS - 1, item_step, (x, r, p, rr))
        g = item_product(p.astype(BF16), q, False) + ridge_item * p
        x = x + (rr / jnp.sum(p * g, axis=0, keepdims=True)) * p
        item_out[pl.ds(pl.multiple_of(row * own_items + q * width, width), width), :] = x.T
        pending.append(gather_own(q))

    for q in range(CHUNKS):
        gather_first(q, pending[q])
    for b in range(4):
        for q in range(CHUNKS):
            gather_second(q, pending[q], b)
    for q in range(CHUNKS):
        for h in range(2):
            for b in range(4):
                for s in range(2):
                    pending[q][h, 3, b, s].wait_recv()
    for c in started:
        c.wait_send()
    w_copy.wait()


def solution(mesh):
    grid_spec = P(("part", "row"), "col")
    user_spec = P(("part", "row"), None)
    item_spec = P(("part", "col"), None)

    def local_step(ratings, mask, user_init, item_init):
        users, items = ratings.shape
        rank = user_init.shape[1]
        own_items = items // NROW
        all_users = users * NROW
        width = own_items // CHUNKS
        half_users = users // 2
        peers = len(OFFSETS)
        dma = pltpu.SemaphoreType.DMA
        hbm = pl.BlockSpec(memory_space=pltpu.HBM)
        vmem = pl.BlockSpec(memory_space=pltpu.VMEM)
        return pl.pallas_call(
            kernel,
            out_shape=(pltpu.VMEM((users, rank), F32), pltpu.VMEM((items, rank), F32)),
            in_specs=[hbm] * 4,
            out_specs=(vmem, vmem),
            scratch_shapes=[
                pltpu.VMEM((users, items), F32),
                pltpu.VMEM((users, items), jnp.int32),
                pltpu.VMEM((items, rank), F32),
                pltpu.VMEM((users, rank), F32),
                pltpu.VMEM((items, rank), BF16),
                pltpu.VMEM((rank, items), BF16),
                pltpu.VMEM((users, items), BF16),
                pltpu.VMEM((CHUNKS, peers, users, width), F32),
                pltpu.VMEM((CHUNKS, all_users, width), F32),
                pltpu.VMEM((CHUNKS, all_users, width), BF16),
                pltpu.VMEM((CG_STEPS + 1, half_users, rank), F32),
                pltpu.VMEM((CG_STEPS + 1, half_users, rank), F32),
                pltpu.VMEM((CG_STEPS + 1, half_users, rank), F32),
                pltpu.VMEM((CG_STEPS + 1, NX - 1, half_users, rank), F32),
                pltpu.VMEM((CG_STEPS, users, rank), BF16),
                pltpu.VMEM((all_users, rank), BF16),
                pltpu.VMEM((rank, all_users), BF16),
                dma((2, NROW)),
                dma,
                dma((8,)),
                dma((CHUNKS, peers)),
                dma((CHUNKS, peers)),
                dma((CG_STEPS + 1,)),
                dma((CG_STEPS + 1,)),
                dma((CG_STEPS + 1, NX - 1)),
                dma((CG_STEPS + 1, NX - 1)),
                dma((CG_STEPS,)),
                dma((CG_STEPS,)),
                dma,
                dma,
                dma((peers,)),
                dma((peers,)),
                dma((NROW,)),
                dma((NROW,)),
                dma((CHUNKS, 2, 20)),
                dma((CHUNKS, 2, 20)),
            ],
            compiler_params=pltpu.CompilerParams(
                collective_id=0, has_side_effects=True, vmem_limit_bytes=48 * 2**20
            ),
            name="als_sweep",
        )(ratings, mask, user_init, item_init)

    return jax.shard_map(
        local_step,
        mesh=mesh,
        in_specs=(grid_spec, grid_spec, user_spec, item_spec),
        out_specs=(user_spec, item_spec),
        check_vma=False,
    )
```

time: 123 us -> 103 us (0.84)
  Pallas kernels: 117 us -> 99.1 us
  local copies, waits for them, and re-layouts: 5.94 us -> 3.48 us
    pallas_call x1, Pallas kernels: 117 us -> 99.1 us  [local_step(): pl.pallas_call(kernel, out_shape=(pltpu.VMEM((users, rank), F32), pltpu.V...]
    unnamed x2 -> x4, local copies, waits for them, and re-layouts: 5.94 us -> 3.48 us
where the time goes in v2:
time: 103 us
  Pallas kernels  99.1 us (96%)
  local copies, waits for them, and re-layouts  3.48 us (3%)
    pallas_call x1, Pallas kernels, local_step(): pl.pallas_call(kernel, out_shape=(pltpu.VMEM((users, rank), F32), pltpu.V...  99.1 us
    unnamed x4, local copies, waits for them, and re-layouts  3.48 us

profile of v2, /device:TPU:0, one launch (start us, length us, event | category | flops | bytes accessed | tf_op | source)
XLA Modules:
  0.0 103.2 jit_solution(17715960816710484262)
XLA Ops:
  0.6 0.0 copy-start
  0.6 0.8 copy-done
  1.5 99.1 %als_sweep.1 = (f32[128,128]{1,0:T(8,128)S(1)}, f32[8192,128]{1,0:T(8,128)S(1)}) custom-call(f32[128,8192]{1,0:T(8,128)} %ratings.1, s32[128,8192]{1,0:T(8,128)} %mask.1, f32[128,128]{1,0:T(8,128)S(1)} %copy-done, f32[8192,128]{1,0:T(8,128)} %item_init.1), custom_call_target="tpu_custom_call" | custom-call | tf_op jit(solution)/shard_map/als_sweep/pallas_call | solution.py:387
  100.6 0.6 copy.8
  101.2 2.0 %copy.9 = f32[8192,128]{1,0:T(8,128)} copy(f32[8192,128]{1,0:T(8,128)S(1)} %get-tuple-element.3) | data formatting | bytes 8388608
Async XLA Ops:
  0.6 0.8 copy-start

commit v3 on v2

--- a/solution.py
+++ b/solution.py
@@ -22,6 +22,7 @@
 NEAR_FIRST = sorted(
     range(len(OFFSETS)), key=lambda k: min(OFFSETS[k][0], NZ - OFFSETS[k][0]) + min(OFFSETS[k][1], NY - OFFSETS[k][1])
 )
+PACE = [(0, 1, 2), (3, 4, 5, 6), (7, 8, 9, 10), (), (11, 12, 13, 14)]
 
 
 def dot(a, b, ca, cb):
@@ -31,7 +32,7 @@
 def kernel(
     ratings, mask, user_init, item_init, user_out, item_out,
     r_in, m_in, v_in, w_in, fixed, fixed_t, mask_bf, r_send, r_recv, mask_items,
-    pair_send, pair_recv, chip_sum, x_recv, p_all, fw, fw_t,
+    masked, pair_send, pair_recv, chip_sum, x_recv, p_all, fw, fw_t,
     in_sem, w_in_sem, v_in_sem, a2a_send, a2a_recv, pair_send_sem, pair_recv_sem, x_send_sem, x_recv_sem,
     ag_send, ag_recv, wc_send, wc_recv, wr_send, wr_recv, wf_send, wf_recv, vg_send, vg_recv,
 ):
@@ -123,20 +124,18 @@
                 exchange_start(j, 0)
         elif k >= ahead and k < len(OFFSETS):
             exchange_start(k, 0)
-    for q in range(1, CHUNKS):
-        for k in range(len(OFFSETS)):
-            exchange_start(k, q)
 
     mine = pl.ds(pl.multiple_of(core * half_users, half_users), half_users)
     other = pl.ds(pl.multiple_of((1 - core) * half_users, half_users), half_users)
-
-    def reduce_users(it, product, meanwhile=None):
-        pair_send[it] = product(other)
+    sides = (other, mine)
+
+    def reduce_users(it, product, meanwhile):
+        pair_send[it] = product(0)
         c = remote(pair_send.at[it], pair_recv.at[it], pair_send_sem.at[it], pair_recv_sem.at[it], partner)
         c.start()
-        own = product(mine)
+        chip_sum[it] = product(1)
         c.wait()
-        own = own + pair_recv[it]
+        own = chip_sum[it] + pair_recv[it]
         chip_sum[it] = own
         copies = []
         for k in (2, 1, 3):
@@ -145,8 +144,7 @@
             )
             c.start()
             copies.append(c)
-        if meanwhile is not None:
-            meanwhile()
+        meanwhile()
         for c in copies:
             c.wait()
         return (own + x_recv[it, 1]) + (x_recv[it, 0] + x_recv[it, 2])
@@ -158,59 +156,64 @@
         c.wait()
 
     def user_product(it):
-        def product(rows):
+        def product(side):
+            rows = sides[side]
             p = p_all[it, rows, :]
-            acc = jnp.zeros((half_users, rank), F32)
             for t in range(8):
                 cols = slice(t * tile, (t + 1) * tile)
-                z = dot(p, fixed_t[:, cols], 1, 0).astype(BF16) * mask_bf[rows, cols]
-                acc = acc + dot(z, fixed[cols, :], 1, 0)
-            return acc
+                masked[side, :, cols] = dot(p, fixed_t[:, cols], 1, 0).astype(BF16) * mask_bf[rows, cols]
+            return dot(masked[side], fixed[...], 1, 0)
         return product
 
     w_load.wait()
-    ready = []
-
-    def user_residual(rows):
-        w = w_in[rows, :].astype(BF16)
-        acc = jnp.zeros((half_users, rank), F32)
-        for t in range(8):
-            cols = slice(t * tile, (t + 1) * tile)
-            if len(ready) <= t:
-                v_loads[t].wait()
-                fixed[cols, :] = v_in[cols, :].astype(BF16)
-                ready.append(t)
-            f = fixed[cols, :]
-            d = jnp.where(m_in[rows, cols] > 0, r_in[rows, cols] - dot(w, f, 1, 1), 0.0).astype(BF16)
-            acc = acc + dot(d, f, 1, 0)
-        return acc
-
-    def transpose_fixed():
-        for t in range(8):
-            cols = slice(t * tile, (t + 1) * tile)
-            fixed_t[:, cols] = fixed[cols, :].T
+    w = w_in[...].astype(BF16)
+    for t in range(8):
+        cols = slice(t * tile, (t + 1) * tile)
+        v_loads[t].wait()
+        f = v_in[cols, :].astype(BF16)
+        fixed[cols, :] = f
+        d = jnp.where(m_in[:, cols] > 0, r_in[:, cols] - dot(w, f, 1, 1), 0.0).astype(BF16)
+        masked[0, :, cols] = d[:half_users]
+        masked[1, :, cols] = d[half_users:]
+
+    def user_residual(side):
+        return dot(masked[lax.rem(core + 1 + side, 2)], fixed[...], 1, 0)
+
+    def item_mask(q):
+        for k in range(len(OFFSETS)):
+            exchange[q, k].wait()
+        for t in range(4):
+            rows = slice(t * tall, (t + 1) * tall)
+            mask_items[q, rows, :] = jnp.where(r_recv[q, rows, :] < jnp.inf, 1.0, 0.0).astype(BF16)
+
+    def meanwhile(it):
+        def work():
+            if it == 0:
+                for t in range(8):
+                    cols = slice(t * tile, (t + 1) * tile)
+                    fixed_t[:, cols] = fixed[cols, :].T
+            else:
+                for k in PACE[it - 1]:
+                    exchange_start(k, 1)
+            if it == CG_STEPS:
+                item_mask(0)
+        return work
 
     x = w_in[mine, :]
-    r = reduce_users(0, user_residual, transpose_fixed) - ridge_user * x
+    r = reduce_users(0, user_residual, meanwhile(0)) - ridge_user * x
     p = r
     rr = jnp.sum(r * r, axis=1, keepdims=True)
     share_direction(0, p)
-
-    def user_step(it, state):
-        x, r, p, rr = state
-        q = reduce_users(it, user_product(it - 1)) + ridge_user * p
+    for it in range(1, CG_STEPS + 1):
+        q = reduce_users(it, user_product(it - 1), meanwhile(it)) + ridge_user * p
         a = rr / jnp.sum(p * q, axis=1, keepdims=True)
         x = x + a * p
-        r = r - a * q
-        rn = jnp.sum(r * r, axis=1, keepdims=True)
-        p = r + (rn / rr) * p
-        share_direction(it, p)
-        return x, r, p, rn
-
-    x, r, p, rr = lax.fori_loop(1, CG_STEPS, user_step, (x, r, p, rr))
-    q = reduce_users(CG_STEPS, user_product(CG_STEPS - 1)) + ridge_user * p
-    a = rr / jnp.sum(p * q, axis=1, keepdims=True)
-    x = x + a * p
+        if it < CG_STEPS:
+            r = r - a * q
+            rn = jnp.sum(r * r, axis=1, keepdims=True)
+            p = r + (rn / rr) * p
+            rr = rn
+            share_direction(it, p)
 
     def user_block(r):
         return pl.ds(pl.multiple_of(r * users + core * half_users, half_users), half_users)
@@ -228,15 +231,10 @@
     w_copy = remote(user_out.at[mine], user_out.at[mine], wc_send, wc_recv, partner)
     w_copy.start()
 
-    def item_mask(q):
-        for k in range(len(OFFSETS)):
-            exchange[q, k].wait()
-        for t in range(4):
-            rows = slice(t * tall, (t + 1) * tall)
-            mask_items[q, rows, :] = jnp.where(r_recv[q, rows, :] < jnp.inf, 1.0, 0.0).astype(BF16)
+    for k in PACE[CG_STEPS]:
+        exchange_start(k, 1)
 
     x_all = v_in[pl.ds(pl.multiple_of(row * own_items, own_items), own_items), :].T
-    item_mask(0)
     sources = [row]
     for k in NEAR_FIRST:
         shared[k].wait()
@@ -245,10 +243,14 @@
         c.start()
         crossed.append(c)
         sources.append(src)
-    for c, src in zip(crossed, sources):
-        c.wait()
-        blk = pl.ds(pl.multiple_of(src * users, users), users)
-        fw_t[:, blk] = fw[blk, :].T
+    done = 0
+    for n in (5, 6, 5):
+        for c in crossed[done:done + n]:
+            c.wait()
+        for src in sources[done:done + n]:
+            blk = pl.ds(pl.multiple_of(src * users, users), users)
+            fw_t[:, blk] = fw[blk, :].T
+        done += n
 
     def item_product(p_bf, q, first):
         acc = jnp.zeros((rank, width), F32)
@@ -400,6 +402,7 @@
                 pltpu.VMEM((CHUNKS, peers, users, width), F32),
                 pltpu.VMEM((CHUNKS, all_users, width), F32),
                 pltpu.VMEM((CHUNKS, all_users, width), BF16),
+                pltpu.VMEM((2, half_users, items), BF16),
                 pltpu.VMEM((CG_STEPS + 1, half_users, rank), F32),
                 pltpu.VMEM((CG_STEPS + 1, half_users, rank), F32),
                 pltpu.VMEM((CG_STEPS + 1, half_users, rank), F32),

time: 103 us -> 97.8 us (0.950)
  Pallas kernels: 99.1 us -> 93.5 us
    pallas_call x1, Pallas kernels: 99.1 us -> 93.5 us  [local_step(): pl.pallas_call(kernel, out_shape=(pltpu.VMEM((users, rank), F32), pltpu.V...]
where the time goes in v3:
time: 97.8 us; the launch traced here: 97.7 us
  Pallas kernels  93.5 us (96%)
  local copies, waits for them, and re-layouts  3.48 us (4%)
    pallas_call x1, Pallas kernels, local_step(): pl.pallas_call(kernel, out_shape=(pltpu.VMEM((users, rank), F32), pltpu.V...  93.5 us
    unnamed x4, local copies, waits for them, and re-layouts  3.48 us

profile of v3, /device:TPU:0, one launch (start us, length us, event | category | flops | bytes accessed | tf_op | source)
XLA Modules:
  0.0 97.7 jit_solution(8255953597967292560)
XLA Ops:
  0.6 0.0 copy-start
  0.6 0.8 copy-done
  1.5 93.5 %als_sweep.1 = (f32[128,128]{1,0:T(8,128)S(1)}, f32[8192,128]{1,0:T(8,128)S(1)}) custom-call(f32[128,8192]{1,0:T(8,128)} %ratings.1, s32[128,8192]{1,0:T(8,128)} %mask.1, f32[128,128]{1,0:T(8,128)S(1)} %copy-done, f32[8192,128]{1,0:T(8,128)} %item_init.1), custom_call_target="tpu_custom_call" | custom-call | tf_op jit(solution)/shard_map/als_sweep/pallas_call | solution.py:389
  95.0 0.6 copy.8
  95.6 2.0 %copy.9 = f32[8192,128]{1,0:T(8,128)} copy(f32[8192,128]{1,0:T(8,128)S(1)} %get-tuple-element.3) | data formatting | bytes 8388608
Async XLA Ops:
  0.6 0.8 copy-start

commit v4 on v3

--- a/solution.py
+++ b/solution.py
@@ -17,12 +17,17 @@
 NCOL = NX * 2
 CHUNKS = 2
 OFFSETS = [
-    (1, 1), (3, 3), (1, 0), (3, 0), (2, 1), (2, 3), (2, 0), (1, 3), (3, 1), (1, 2), (3, 2), (2, 2), (0, 1), (0, 3), (0, 2),
+    (1, 1), (3, 3), (3, 1), (1, 3), (0, 1), (2, 3), (2, 1), (0, 3), (2, 2), (1, 2), (3, 2), (0, 2), (1, 0), (3, 0), (2, 0),
 ]
 NEAR_FIRST = sorted(
     range(len(OFFSETS)), key=lambda k: min(OFFSETS[k][0], NZ - OFFSETS[k][0]) + min(OFFSETS[k][1], NY - OFFSETS[k][1])
 )
-PACE = [(0, 1, 2), (3, 4, 5, 6), (7, 8, 9, 10), (), (11, 12, 13, 14)]
+SLOT = {k: n + 1 for n, k in enumerate(NEAR_FIRST)}
+PACE = [(), (), (0, 1, 2, 3), (4, 5, 6, 7), (8, 9, 10, 11, 12, 13, 14)]
+
+
+def chunk_starts(own_items):
+    return (0, own_items // 4, own_items)
 
 
 def dot(a, b, ca, cb):
@@ -31,8 +36,8 @@
 
 def kernel(
     ratings, mask, user_init, item_init, user_out, item_out,
-    r_in, m_in, v_in, w_in, fixed, fixed_t, mask_bf, r_send, r_recv, mask_items,
-    masked, pair_send, pair_recv, chip_sum, x_recv, p_all, fw, fw_t,
+    r_in, m_in, v_in, w_in, fixed, fixed_t, mask_bf, r_send0, r_send1, r_recv0, r_recv1, mask0, mask1, item_masked,
+    masked, pair_send, pair_recv, chip_sum, x_recv, p_all, fw, fw_t, x_items,
     in_sem, w_in_sem, v_in_sem, a2a_send, a2a_recv, pair_send_sem, pair_recv_sem, x_send_sem, x_recv_sem,
     ag_send, ag_recv, wc_send, wc_recv, wr_send, wr_recv, wf_send, wf_recv, vg_send, vg_recv,
 ):
@@ -41,8 +46,9 @@
     half_users = users // 2
     own_items = items // NROW
     all_users = users * NROW
-    width = own_items // CHUNKS
-    half = width // 2
+    starts = chunk_starts(own_items)
+    widths = [starts[q + 1] - starts[q] for q in range(CHUNKS)]
+    r_send, r_recv, mask_items = (r_send0, r_send1), (r_recv0, r_recv1), (mask0, mask1)
     tall = all_users // 4
     tile = items // 8
     row = lax.axis_index("row")
@@ -93,17 +99,17 @@
         c.start()
         v_loads.append(c)
 
-    my_users = pl.ds(pl.multiple_of(row * users, users), users)
     exchange = {}
 
-    def exchange_start(k, q):
+    def exchange_start(k, q, part):
         dz, dy = order[k]
+        rows, n = ((0, users), (0, half_users), (half_users, half_users))[part]
         c = remote(
-            r_send.at[q, k], r_recv.at[q, my_users, :], a2a_send.at[q, k], a2a_recv.at[q, k],
-            row_dev(row_of(dz, dy)),
+            r_send[q].at[k, pl.ds(rows, n)], r_recv[q].at[pl.ds(SLOT[k] * users + rows, n)],
+            a2a_send.at[part, k], a2a_recv.at[part, k], row_dev(row_of(dz, dy)),
         )
         c.start()
-        exchange[q, k] = c
+        exchange[part, k] = c
 
     ahead = 4
     for k, (dz, dy) in enumerate(order):
@@ -115,15 +121,17 @@
         marked = jnp.where(on, r_in[:, cols], jnp.inf)
         for q in range(CHUNKS):
             if (dz, dy) == (0, 0):
-                r_recv[q, my_users, :] = marked[:, q * width:(q + 1) * width]
+                r_recv[q][0:users, :] = marked[:, starts[q]:starts[q + 1]]
             else:
-                r_send[q, k] = marked[:, q * width:(q + 1) * width]
+                r_send[q][k] = marked[:, starts[q]:starts[q + 1]]
         if k == ahead - 1:
             pl.semaphore_wait(barrier, len(peers))
             for j in range(ahead):
-                exchange_start(j, 0)
+                exchange_start(j, 0, 0)
         elif k >= ahead and k < len(OFFSETS):
-            exchange_start(k, 0)
+            exchange_start(k, 0, 0)
+    for k in range(len(OFFSETS)):
+        exchange_start(k, 1, 1)
 
     mine = pl.ds(pl.multiple_of(core * half_users, half_users), half_users)
     other = pl.ds(pl.multiple_of((1 - core) * half_users, half_users), half_users)
@@ -180,11 +188,12 @@
         return dot(masked[lax.rem(core + 1 + side, 2)], fixed[...], 1, 0)
 
     def item_mask(q):
-        for k in range(len(OFFSETS)):
-            exchange[q, k].wait()
+        for part in (0,) if q == 0 else (1, 2):
+            for k in range(len(OFFSETS)):
+                exchange[part, k].wait()
         for t in range(4):
             rows = slice(t * tall, (t + 1) * tall)
-            mask_items[q, rows, :] = jnp.where(r_recv[q, rows, :] < jnp.inf, 1.0, 0.0).astype(BF16)
+            mask_items[q][rows, :] = jnp.where(r_recv[q][rows, :] < jnp.inf, 1.0, 0.0).astype(BF16)
 
     def meanwhile(it):
         def work():
@@ -194,8 +203,9 @@
                     fixed_t[:, cols] = fixed[cols, :].T
             else:
                 for k in PACE[it - 1]:
-                    exchange_start(k, 1)
-            if it == CG_STEPS:
+                    exchange_start(k, 1, 2)
+            if it == 2:
+                x_items[...] = v_in[pl.ds(pl.multiple_of(row * own_items, own_items), own_items), :].T
                 item_mask(0)
         return work
 
@@ -215,62 +225,63 @@
             rr = rn
             share_direction(it, p)
 
-    def user_block(r):
-        return pl.ds(pl.multiple_of(r * users + core * half_users, half_users), half_users)
-
-    fw[user_block(row), :] = x.astype(BF16)
+    def user_block(slot):
+        return pl.ds(pl.multiple_of(slot * users + core * half_users, half_users), half_users)
+
+    fw[user_block(0), :] = x.astype(BF16)
     shared = {}
     for k in reversed(NEAR_FIRST):
-        blk = user_block(row)
-        c = remote(fw.at[blk], fw.at[blk], wr_send.at[k], wr_recv.at[k], row_dev(row_of(*OFFSETS[k])))
-        c.start()
-        shared[k] = c
-    crossed = [remote(fw.at[user_block(row)], fw.at[user_block(row)], wf_send.at[NROW - 1], wf_recv.at[NROW - 1], partner)]
-    crossed[0].start()
+        c = remote(
+            fw.at[user_block(0)], fw.at[user_block(SLOT[k])], wr_send.at[k], wr_recv.at[k],
+            row_dev(row_of(*OFFSETS[k])),
+        )
+        c.start()
+        shared[SLOT[k]] = c
+    crossed = {}
+
+    def cross(slot):
+        blk = user_block(slot)
+        crossed[slot] = remote(fw.at[blk], fw.at[blk], wf_send.at[slot], wf_recv.at[slot], partner)
+        crossed[slot].start()
+
+    cross(0)
     user_out[mine, :] = x
     w_copy = remote(user_out.at[mine], user_out.at[mine], wc_send, wc_recv, partner)
     w_copy.start()
-
     for k in PACE[CG_STEPS]:
-        exchange_start(k, 1)
-
-    x_all = v_in[pl.ds(pl.multiple_of(row * own_items, own_items), own_items), :].T
-    sources = [row]
-    for k in NEAR_FIRST:
-        shared[k].wait()
-        src = row_of(NZ - OFFSETS[k][0], NY - OFFSETS[k][1])
-        c = remote(fw.at[user_block(src)], fw.at[user_block(src)], wf_send.at[k], wf_recv.at[k], partner)
-        c.start()
-        crossed.append(c)
-        sources.append(src)
-    done = 0
-    for n in (5, 6, 5):
-        for c in crossed[done:done + n]:
-            c.wait()
-        for src in sources[done:done + n]:
-            blk = pl.ds(pl.multiple_of(src * users, users), users)
-            fw_t[:, blk] = fw[blk, :].T
-        done += n
-
-    def item_product(p_bf, q, first):
-        acc = jnp.zeros((rank, width), F32)
+        exchange_start(k, 1, 2)
+
+    def arrive(t):
+        for slot in range(4 * t, 4 * t + 4):
+            if slot:
+                shared[slot].wait()
+                cross(slot)
+
+    def settle(t):
+        for slot in range(4 * t, 4 * t + 4):
+            crossed[slot].wait()
+        rows = slice(t * tall, (t + 1) * tall)
+        fw_t[:, rows] = fw[rows, :].T
+
+    def item_residual(p_bf, q, t):
+        rows = slice(t * tall, (t + 1) * tall)
+        known = r_recv[q][rows, :]
+        z = jnp.where(known < jnp.inf, known - dot(fw[rows, :], p_bf, 1, 0), 0.0).astype(BF16)
+        return dot(fw_t[:, rows], z, 1, 0)
+
+    def item_product(p_bf, q):
         for t in range(4):
             rows = slice(t * tall, (t + 1) * tall)
-            s = dot(fw[rows, :], p_bf, 1, 0)
-            if first:
-                known = r_recv[q, rows, :]
-                z = jnp.where(known < jnp.inf, known - s, 0.0).astype(BF16)
-            else:
-                z = s.astype(BF16) * mask_items[q, rows, :]
-            acc = acc + dot(fw_t[:, rows], z, 1, 0)
-        return acc
+            item_masked[rows, :widths[q]] = dot(fw[rows, :], p_bf, 1, 0).astype(BF16) * mask_items[q][rows, :]
+        return dot(fw_t[...], item_masked[:, :widths[q]], 1, 0)
 
     def block(r, q, h):
-        return pl.ds(pl.multiple_of(r * own_items + q * width + h * half, half), half)
+        n = widths[q] // 2
+        return pl.ds(pl.multiple_of(r * own_items + starts[q] + h * n, 64), n)
 
     def halfblock(r, q, h, part):
-        n = half // 2
-        return pl.ds(pl.multiple_of(r * own_items + q * width + h * half + part * n, n), n)
+        n = widths[q] // 4
+        return pl.ds(pl.multiple_of(r * own_items + starts[q] + (2 * h + part) * n, 32), n)
 
     dims = [((0, 1), (1, 0)), ((1, 0), (0, 1))]
 
@@ -334,14 +345,24 @@
     for q in range(CHUNKS):
         if q:
             item_mask(q)
-        x = x_all[:, q * width:(q + 1) * width]
-        r = item_product(x.astype(BF16), q, True) - ridge_item * x
+        x = x_items[:, starts[q]:starts[q + 1]]
+        x_bf = x.astype(BF16)
+        r = -ridge_item * x
+        if q == 0:
+            arrive(0)
+            arrive(1)
+        for t in range(4):
+            if q == 0:
+                settle(t)
+            r = r + item_residual(x_bf, q, t)
+            if q == 0 and t < 2:
+                arrive(t + 2)
         p = r
         rr = jnp.sum(r * r, axis=0, keepdims=True)
 
         def item_step(_, state):
             x, r, p, rr = state
-            g = item_product(p.astype(BF16), q, False) + ridge_item * p
+            g = item_product(p.astype(BF16), q) + ridge_item * p
             a = rr / jnp.sum(p * g, axis=0, keepdims=True)
             x = x + a * p
             r = r - a * g
@@ -350,9 +371,10 @@
             return x, r, p, rn
 
         x, r, p, rr = lax.fori_loop(0, CG_STEPS - 1, item_step, (x, r, p, rr))
-        g = item_product(p.astype(BF16), q, False) + ridge_item * p
+        g = item_product(p.astype(BF16), q) + ridge_item * p
         x = x + (rr / jnp.sum(p * g, axis=0, keepdims=True)) * p
-        item_out[pl.ds(pl.multiple_of(row * own_items + q * width, width), width), :] = x.T
+        first = pl.multiple_of(row * own_items + starts[q], widths[0])
+        item_out[pl.ds(first, widths[q]), :] = x.T
         pending.append(gather_own(q))
 
     for q in range(CHUNKS):
@@ -380,7 +402,8 @@
         rank = user_init.shape[1]
         own_items = items // NROW
         all_users = users * NROW
-        width = own_items // CHUNKS
+        starts = chunk_starts(own_items)
+        widths = [starts[q + 1] - starts[q] for q in range(CHUNKS)]
         half_users = users // 2
         peers = len(OFFSETS)
         dma = pltpu.SemaphoreType.DMA
@@ -399,9 +422,10 @@
                 pltpu.VMEM((items, rank), BF16),
                 pltpu.VMEM((rank, items), BF16),
                 pltpu.VMEM((users, items), BF16),
-                pltpu.VMEM((CHUNKS, peers, users, width), F32),
-                pltpu.VMEM((CHUNKS, all_users, width), F32),
-                pltpu.VMEM((CHUNKS, all_users, width), BF16),
+                *[pltpu.VMEM((peers, users, w), F32) for w in widths],
+                *[pltpu.VMEM((all_users, w), F32) for w in widths],
+                *[pltpu.VMEM((all_users, w), BF16) for w in widths],
+                pltpu.VMEM((all_users, widths[-1]), BF16),
                 pltpu.VMEM((2, half_users, items), BF16),
                 pltpu.VMEM((CG_STEPS + 1, half_users, rank), F32),
                 pltpu.VMEM((CG_STEPS + 1, half_users, rank), F32),
@@ -410,11 +434,12 @@
                 pltpu.VMEM((CG_STEPS, users, rank), BF16),
                 pltpu.VMEM((all_users, rank), BF16),
                 pltpu.VMEM((rank, all_users), BF16),
+                pltpu.VMEM((rank, own_items), F32),
                 dma((2, NROW)),
                 dma,
                 dma((8,)),
-                dma((CHUNKS, peers)),
-                dma((CHUNKS, peers)),
+                dma((3, peers)),
+                dma((3, peers)),
                 dma((CG_STEPS + 1,)),
                 dma((CG_STEPS + 1,)),
                 dma((CG_STEPS + 1, NX - 1)),
@@ -434,7 +459,7 @@
                 collective_id=0, has_side_effects=True, vmem_limit_bytes=48 * 2**20
             ),
             name="als_sweep",
-        )(ratings, mask, user_init, item_init)
+        )(ratings, mask, pltpu.with_memory_space_constraint(user_init, pltpu.HBM), item_init)
 
     return jax.shard_map(
         local_step,

time: 97.8 us -> 103 us (1.053)
  Pallas kernels: 93.5 us -> 100 us
    pallas_call x1, Pallas kernels: 93.5 us -> 100 us  [local_step(): pl.pallas_call(kernel, out_shape=(pltpu.VMEM((users, rank), F32), pltpu.V...]
    unnamed x4 -> x2, local copies, waits for them, and re-layouts: 3.48 us -> 2.64 us
where the time goes in v4:
time: 103 us
  Pallas kernels  100 us (97%)
  local copies, waits for them, and re-layouts  2.64 us (3%)
    pallas_call x1, Pallas kernels, local_step(): pl.pallas_call(kernel, out_shape=(pltpu.VMEM((users, rank), F32), pltpu.V...  100 us
    unnamed x2, local copies, waits for them, and re-layouts  2.64 us

profile of v4, /device:TPU:0, one launch (start us, length us, event | category | flops | bytes accessed | tf_op | source)
XLA Modules:
  0.0 103.3 jit_solution(8903162644484020015)
XLA Ops:
  0.6 100.0 %als_sweep.1 = (f32[128,128]{1,0:T(8,128)S(1)}, f32[8192,128]{1,0:T(8,128)S(1)}) custom-call(f32[128,8192]{1,0:T(8,128)} %ratings.1, s32[128,8192]{1,0:T(8,128)} %mask.1, f32[128,128]{1,0:T(8,128)} %user_init.1, f32[8192,128]{1,0:T(8,128)} %item_init.1), custom_call_target="tpu_custom_call" | custom-call | tf_op jit(solution)/shard_map/als_sweep/pallas_call | solution.py:412
  100.6 0.6 copy.8
  101.3 2.0 %copy.9 = f32[8192,128]{1,0:T(8,128)} copy(f32[8192,128]{1,0:T(8,128)S(1)} %get-tuple-element.3) | data formatting | bytes 8388608

commit v5 on v4

--- a/solution.py
+++ b/solution.py
@@ -23,11 +23,11 @@
     range(len(OFFSETS)), key=lambda k: min(OFFSETS[k][0], NZ - OFFSETS[k][0]) + min(OFFSETS[k][1], NY - OFFSETS[k][1])
 )
 SLOT = {k: n + 1 for n, k in enumerate(NEAR_FIRST)}
-PACE = [(), (), (0, 1, 2, 3), (4, 5, 6, 7), (8, 9, 10, 11, 12, 13, 14)]
+PACE = [(), (), (), (), tuple(range(15))]
 
 
 def chunk_starts(own_items):
-    return (0, own_items // 4, own_items)
+    return (0, own_items * 3 // 4, own_items)
 
 
 def dot(a, b, ca, cb):
@@ -101,15 +101,14 @@
 
     exchange = {}
 
-    def exchange_start(k, q, part):
+    def exchange_start(k, q):
         dz, dy = order[k]
-        rows, n = ((0, users), (0, half_users), (half_users, half_users))[part]
         c = remote(
-            r_send[q].at[k, pl.ds(rows, n)], r_recv[q].at[pl.ds(SLOT[k] * users + rows, n)],
-            a2a_send.at[part, k], a2a_recv.at[part, k], row_dev(row_of(dz, dy)),
+            r_send[q].at[k], r_recv[q].at[pl.ds(SLOT[k] * users, users)],
+            a2a_send.at[q, k], a2a_recv.at[q, k], row_dev(row_of(dz, dy)),
         )
         c.start()
-        exchange[part, k] = c
+        exchange[q, k] = c
 
     ahead = 4
     for k, (dz, dy) in enumerate(order):
@@ -127,11 +126,9 @@
         if k == ahead - 1:
             pl.semaphore_wait(barrier, len(peers))
             for j in range(ahead):
-                exchange_start(j, 0, 0)
+                exchange_start(j, 0)
         elif k >= ahead and k < len(OFFSETS):
-            exchange_start(k, 0, 0)
-    for k in range(len(OFFSETS)):
-        exchange_start(k, 1, 1)
+            exchange_start(k, 0)
 
     mine = pl.ds(pl.multiple_of(core * half_users, half_users), half_users)
     other = pl.ds(pl.multiple_of((1 - core) * half_users, half_users), half_users)
@@ -188,9 +185,8 @@
         return dot(masked[lax.rem(core + 1 + side, 2)], fixed[...], 1, 0)
 
     def item_mask(q):
-        for part in (0,) if q == 0 else (1, 2):
-            for k in range(len(OFFSETS)):
-                exchange[part, k].wait()
+        for k in range(len(OFFSETS)):
+            exchange[q, k].wait()
         for t in range(4):
             rows = slice(t * tall, (t + 1) * tall)
             mask_items[q][rows, :] = jnp.where(r_recv[q][rows, :] < jnp.inf, 1.0, 0.0).astype(BF16)
@@ -203,8 +199,8 @@
                     fixed_t[:, cols] = fixed[cols, :].T
             else:
                 for k in PACE[it - 1]:
-                    exchange_start(k, 1, 2)
-            if it == 2:
+                    exchange_start(k, 1)
+            if it == CG_STEPS:
                 x_items[...] = v_in[pl.ds(pl.multiple_of(row * own_items, own_items), own_items), :].T
                 item_mask(0)
         return work
@@ -249,7 +245,7 @@
     w_copy = remote(user_out.at[mine], user_out.at[mine], wc_send, wc_recv, partner)
     w_copy.start()
     for k in PACE[CG_STEPS]:
-        exchange_start(k, 1, 2)
+        exchange_start(k, 1)
 
     def arrive(t):
         for slot in range(4 * t, 4 * t + 4):
@@ -373,7 +369,7 @@
         x, r, p, rr = lax.fori_loop(0, CG_STEPS - 1, item_step, (x, r, p, rr))
         g = item_product(p.astype(BF16), q) + ridge_item * p
         x = x + (rr / jnp.sum(p * g, axis=0, keepdims=True)) * p
-        first = pl.multiple_of(row * own_items + starts[q], widths[0])
+        first = pl.multiple_of(row * own_items + starts[q], 128)
         item_out[pl.ds(first, widths[q]), :] = x.T
         pending.append(gather_own(q))
 
@@ -425,7 +421,7 @@
                 *[pltpu.VMEM((peers, users, w), F32) for w in widths],
                 *[pltpu.VMEM((all_users, w), F32) for w in widths],
                 *[pltpu.VMEM((all_users, w), BF16) for w in widths],
-                pltpu.VMEM((all_users, widths[-1]), BF16),
+                pltpu.VMEM((all_users, max(widths)), BF16),
                 pltpu.VMEM((2, half_users, items), BF16),
                 pltpu.VMEM((CG_STEPS + 1, half_users, rank), F32),
                 pltpu.VMEM((CG_STEPS + 1, half_users, rank), F32),
@@ -438,8 +434,8 @@
                 dma((2, NROW)),
                 dma,
                 dma((8,)),
-                dma((3, peers)),
-                dma((3, peers)),
+                dma((CHUNKS, peers)),
+                dma((CHUNKS, peers)),
                 dma((CG_STEPS + 1,)),
                 dma((CG_STEPS + 1,)),
                 dma((CG_STEPS + 1, NX - 1)),

time: 103 us -> 92.8 us (0.901)
  Pallas kernels: 100 us -> 89.4 us
    pallas_call x1, Pallas kernels: 100 us -> 89.4 us  [local_step(): pl.pallas_call(kernel, out_shape=(pltpu.VMEM((users, rank), F32), pltpu.V...]
where the time goes in v5:
time: 92.8 us; the launch traced here: 92.7 us
  Pallas kernels  89.4 us (96%)
  local copies, waits for them, and re-layouts  2.64 us (3%)
    pallas_call x1, Pallas kernels, local_step(): pl.pallas_call(kernel, out_shape=(pltpu.VMEM((users, rank), F32), pltpu.V...  89.4 us
    unnamed x2, local copies, waits for them, and re-layouts  2.64 us

profile of v5, /device:TPU:0, one launch (start us, length us, event | category | flops | bytes accessed | tf_op | source)
XLA Modules:
  0.0 92.7 jit_solution(323843500267570316)
XLA Ops:
  0.6 89.4 %als_sweep.1 = (f32[128,128]{1,0:T(8,128)S(1)}, f32[8192,128]{1,0:T(8,128)S(1)}) custom-call(f32[128,8192]{1,0:T(8,128)} %ratings.1, s32[128,8192]{1,0:T(8,128)} %mask.1, f32[128,128]{1,0:T(8,128)} %user_init.1, f32[8192,128]{1,0:T(8,128)} %item_init.1), custom_call_target="tpu_custom_call" | custom-call | tf_op jit(solution)/shard_map/als_sweep/pallas_call | solution.py:408
  90.0 0.6 copy.8
  90.7 2.0 %copy.9 = f32[8192,128]{1,0:T(8,128)} copy(f32[8192,128]{1,0:T(8,128)S(1)} %get-tuple-element.3) | data formatting | bytes 8388608

commit v6 on v5

--- a/solution.py
+++ b/solution.py
@@ -17,7 +17,7 @@
 NCOL = NX * 2
 CHUNKS = 2
 OFFSETS = [
-    (1, 1), (3, 3), (3, 1), (1, 3), (0, 1), (2, 3), (2, 1), (0, 3), (2, 2), (1, 2), (3, 2), (0, 2), (1, 0), (3, 0), (2, 0),
+    (1, 1), (3, 3), (1, 0), (3, 0), (2, 1), (2, 3), (2, 0), (1, 3), (3, 1), (1, 2), (3, 2), (2, 2), (0, 1), (0, 3), (0, 2),
 ]
 NEAR_FIRST = sorted(
     range(len(OFFSETS)), key=lambda k: min(OFFSETS[k][0], NZ - OFFSETS[k][0]) + min(OFFSETS[k][1], NY - OFFSETS[k][1])

time: 92.8 us -> 98 us (1.056)
  Pallas kernels: 89.4 us -> 94.6 us
    pallas_call x1, Pallas kernels: 89.4 us -> 94.6 us  [local_step(): pl.pallas_call(kernel, out_shape=(pltpu.VMEM((users, rank), F32), pltpu.V...]
where the time goes in v6:
time: 98 us; the launch traced here: 97.9 us
  Pallas kernels  94.6 us (97%)
  local copies, waits for them, and re-layouts  2.64 us (3%)
    pallas_call x1, Pallas kernels, local_step(): pl.pallas_call(kernel, out_shape=(pltpu.VMEM((users, rank), F32), pltpu.V...  94.6 us
    unnamed x2, local copies, waits for them, and re-layouts  2.64 us

profile of v6, /device:TPU:0, one launch (start us, length us, event | category | flops | bytes accessed | tf_op | source)
XLA Modules:
  0.0 97.9 jit_solution(16506618324492493839)
XLA Ops:
  0.6 94.6 %als_sweep.1 = (f32[128,128]{1,0:T(8,128)S(1)}, f32[8192,128]{1,0:T(8,128)S(1)}) custom-call(f32[128,8192]{1,0:T(8,128)} %ratings.1, s32[128,8192]{1,0:T(8,128)} %mask.1, f32[128,128]{1,0:T(8,128)} %user_init.1, f32[8192,128]{1,0:T(8,128)} %item_init.1), custom_call_target="tpu_custom_call" | custom-call | tf_op jit(solution)/shard_map/als_sweep/pallas_call | solution.py:408
  95.2 0.6 copy.8
  95.8 2.0 %copy.9 = f32[8192,128]{1,0:T(8,128)} copy(f32[8192,128]{1,0:T(8,128)S(1)} %get-tuple-element.3) | data formatting | bytes 8388608
